TPU v7x, 32 devices: a whole 2x2x4 slice. The times are simulated.
32 devices in a mesh: graphs: 2 (over y), rows: 4 (over z), cols: 2 (over x), sub: 2 (over core).
Axes of the slice: x: 2, y: 2, z: 4, core: 2. Of those that a mesh axis runs over, the one named last changes fastest.
Arguments:
- current_block: float32 [16, 65536], P(None, ('graphs', 'rows', 'cols', 'sub')), parts along dimension 1, may hold values from -1200 to 1200, as said below
- previous_block: float32 [16, 65536], P(None, ('graphs', 'rows', 'cols', 'sub')), parts along dimension 1, may hold values from -1200 to 1200, as said below
- adjacency_tiles: float32 [1536, 128, 128], P(('graphs', 'rows', 'cols', 'sub')), parts along dimension 0, may hold values from -0.3125 to 0.3125
- tile_rows: int32 [1536], P(('graphs', 'rows', 'cols', 'sub')), parts along dimension 0, may hold values from 0 to 255, as said below
- tile_cols: int32 [1536], P(('graphs', 'rows', 'cols', 'sub')), parts along dimension 0, may hold values from 0 to 255, as said below
- tile_count: int32 [32], P(('graphs', 'rows', 'cols', 'sub')), parts along dimension 0, may hold values from 18 to 48, as said below
- locked: int32 [2], P('graphs'), parts along dimension 0, may hold values from 0 to 7
Outputs:
- w_basis: float32 [16, 65536], P(None, ('graphs', 'rows', 'cols', 'sub')), parts along dimension 1
- w_image: float32 [16, 65536], P(None, ('graphs', 'rows', 'cols', 'sub')), parts along dimension 1
- ritz_matrix: float32 [96, 48], P('graphs'), parts along dimension 0
There are 2 independent parts, one for each index of `graphs`. A program takes and returns all parts, laid end to end along the dimension named above; each array names one. Nothing has to cross between parts.
Inputs may be any that keep to these rules, and one draw needn't show every extreme that they name: `current_block`: entries of order one to some hundreds. `previous_block`: entries of order one to some hundreds. Slots d * 48 to (d + 1) * 48 - 1 belong to device d and name its own tile rows d * 16 to (d + 1) * 16 - 1. The first 16 slots of a device name its tile rows in order, with tile_cols equal to tile_rows. Slots past the device's count name tile row d * 16 and carry no weight. `tile_cols`: A slot of device d names a tile column from d * 16 - 8 to (d + 1) * 16 + 7. Slot 16 of a device names a tile of the block before it and slot 17 one of the block after it, where such a block exists. A pair of tile row and tile column may stand in several slots; their tiles add. `tile_count`: in every draw some device has all 48 slots live.
All inputs are finite; a program needn't handle non-finite values.
Results may differ from a plain program's by a relative error of at most 0.000094.
Values sent between devices are 32-bit elements; how exact they have to be, the bound alone decides.
No kernel may reach another device: no remote copies, remote signals or barrier semaphores. Data moves between devices by JAX's collectives and lax.ppermute only.
A program may use at most 64 MiB of HBM per device.

v0:
```python
import jax
import jax.numpy as jnp
from jax import lax
from jax.sharding import PartitionSpec as P


def extended(cells, sides, width):
    for axis, dim in sides:
        count = lax.axis_size(axis)
        ends = count - 1
        head = lax.slice_in_dim(cells, 0, width, axis=dim)
        tail = lax.slice_in_dim(cells, cells.shape[dim] - width, cells.shape[dim], axis=dim)
        cells = jnp.concatenate(
            [
                lax.ppermute(tail, axis, [(i, (i + 1) % count) for i in range(ends)]),
                cells,
                lax.ppermute(head, axis, [((i + 1) % count, i) for i in range(ends)]),
            ],
            axis=dim,
        )
    return cells


def inner_products(left, right):
    return jnp.dot(left, right.T, precision=lax.Precision.HIGHEST)


def solve_lower(factor, values):
    return lax.linalg.triangular_solve(factor, values, left_side=True, lower=True)


def rayleigh_ritz(gram_b, gram_a):
    factor_b = jnp.linalg.cholesky(gram_b)
    symmetric = 0.5 * (gram_a + gram_a.T)
    halfway = solve_lower(factor_b, symmetric)
    return solve_lower(factor_b, halfway.T)


def operate(vectors, padded, adjacency_tiles, column_position, placing, span_tiles):
    channels, rows_here = vectors.shape
    tile_size = adjacency_tiles.shape[1]
    column_blocks = padded.reshape(channels, span_tiles, tile_size)
    gathered = jnp.take(column_blocks, column_position, axis=1)
    products = jnp.einsum(
        "cta,tab->ctb", gathered, adjacency_tiles, precision=lax.Precision.HIGHEST
    )
    summed = jnp.einsum("ctb,tr->crb", products, placing, precision=lax.Precision.HIGHEST)
    return vectors - summed.reshape(channels, rows_here)


def body(current_block, previous_block, adjacency_tiles, tile_rows, tile_cols, tile_count, locked):
    vectors_k, rows_here = current_block.shape
    tile_size = adjacency_tiles.shape[1]
    row_tiles = rows_here // tile_size
    slot_count = adjacency_tiles.shape[0]
    vertex_total = rows_here * lax.axis_size(("rows", "cols", "sub"))
    position = lax.axis_index(("rows", "cols", "sub"))
    reach_tiles = row_tiles // 2
    span_tiles = row_tiles + 2 * reach_tiles
    column_position = tile_cols - (position * row_tiles - reach_tiles)
    row_slot = tile_rows - position * row_tiles
    live_mask = (jnp.arange(slot_count, dtype=jnp.int32) < tile_count[0]).astype(jnp.float32)
    placing = (row_slot[:, None] == jnp.arange(row_tiles, dtype=jnp.int32)[None, :]).astype(
        jnp.float32
    )
    placing = placing * live_mask[:, None]
    stacked = jnp.concatenate([current_block, previous_block], axis=0)
    padded_pair = extended(stacked, ((("rows", "cols", "sub"), 1),), reach_tiles * tile_size)
    pair_image = operate(
        stacked, padded_pair, adjacency_tiles, column_position, placing, span_tiles
    )
    x_image = pair_image[:vectors_k]
    p_image = pair_image[vectors_k:]
    frozen_rows = jnp.arange(vectors_k, dtype=jnp.int32) < locked[0]
    frozen_diag = jnp.diag(frozen_rows.astype(jnp.float32))
    zero_rows = jnp.zeros((vectors_k,), jnp.float32)
    pad_diag = jnp.diag(jnp.concatenate([zero_rows, frozen_rows.astype(jnp.float32), zero_rows]))
    cross_sum, square_sum = lax.psum(
        (jnp.sum(current_block * x_image, axis=1), jnp.sum(current_block * current_block, axis=1)),
        ("rows", "cols", "sub"),
    )
    quotient = cross_sum / (square_sum + 1e-06)
    residual = jnp.where(frozen_rows[:, None], 0.0, x_image - quotient[:, None] * current_block)
    gram_w = (
        lax.psum(inner_products(residual, residual), ("rows", "cols", "sub")) / vertex_total
        + frozen_diag
    )
    factor = jnp.linalg.cholesky(gram_w)
    w_basis = solve_lower(factor, residual)
    padded = extended(w_basis, ((("rows", "cols", "sub"), 1),), reach_tiles * tile_size)
    w_image = operate(w_basis, padded, adjacency_tiles, column_position, placing, span_tiles)
    search = jnp.concatenate([current_block, w_basis, previous_block], axis=0)
    search_image = jnp.concatenate([x_image, w_image, p_image], axis=0)
    plain_sum, image_sum = lax.psum(
        (inner_products(search, search), inner_products(search, search_image)),
        ("rows", "cols", "sub"),
    )
    gram_b = plain_sum / vertex_total + pad_diag
    gram_a = image_sum / vertex_total
    ritz_matrix = rayleigh_ritz(gram_b, gram_a)
    return (w_basis, w_image, ritz_matrix)


def solution(mesh):
    in_specs = (
        P(None, ("graphs", "rows", "cols", "sub")),
        P(None, ("graphs", "rows", "cols", "sub")),
        P(("graphs", "rows", "cols", "sub"), None, None),
        P(("graphs", "rows", "cols", "sub")),
        P(("graphs", "rows", "cols", "sub")),
        P(("graphs", "rows", "cols", "sub")),
        P("graphs"),
    )
    out_specs = (
        P(None, ("graphs", "rows", "cols", "sub")),
        P(None, ("graphs", "rows", "cols", "sub")),
        P("graphs", None),
    )
    return jax.shard_map(body, mesh=mesh, in_specs=in_specs, out_specs=out_specs, check_vma=False)
```

profile of v0, /device:TPU:0, one launch (start us, length us, event | category | flops | bytes accessed | tf_op | source)
XLA Modules:
  0.0 182.3 jit_solution(9188400379763008146)
XLA Ops:
  0.6 1.1 constant_dynamic-update-slice_fusion.1
  1.7 0.9 constant_dynamic-update-slice_fusion
  2.6 0.7 fusion.54
  3.3 3.0 %collective-permute-start = (f32[32,1024]{1,0:T(8,128)}, f32[32,1024]{1,0:T(8,128)}, u32[]{:S(2)}, u32[]{:S(2)}) collective-permute-start(f32[32,1024]{1,0:T(8,128)} %get-tuple-element.14), channel_id=1, source_target_pairs={{0,1},{1,2},{2,3},{3,4},{4,5},{5,6},{6,7},{7,8},{8,9},{9,10},{10,1... | collective-permute-start | bytes 393224 | tf_op jit(solution)/shard_map/ppermute | solution.py:15
  6.4 1.3 collective-permute-start.1
  7.7 0.7 broadcast_subtract_fusion
  10.1 0.7 compare_and_fusion
  11.5 1.8 %copy_bitcast_fusion = f32[32,32,128]{2,0,1:T(8,128)} fusion(f32[32,1024]{1,0:T(8,128)} %collective-permute-done.1, f32[32,2048]{1,0:T(8,128)S(1)} %constant_dynamic-update-slice_fusion, f32[32,1024]{1,0:T(8,128)} %collective-permute-done), kind=kLoop, calls=%fused_computation.9 | loop fusion | flops 262144 | bytes 1048576 | tf_op jit(solution)/shard_map/reshape | solution.py:42
  13.3 2.5 %gather_fusion = f32[48,32,128]{2,1,0:T(8,128)} fusion(f32[32,32,128]{2,0,1:T(8,128)} %copy_bitcast_fusion, s32[1024]{0:T(1024)S(1)} %pad_clamp_fusion), kind=kCustom, calls=%fused_computation | custom fusion | bytes 1573056 | tf_op jit(solution)/shard_map/jit(_take)/gather | solution.py:43
  15.8 4.0 %fusion.2 = f32[48,32,128]{2,1,0:T(8,128)S(1)} fusion(f32[48,128,128]{2,1,0:T(8,128)S(1)} %copy-done, f32[48,32,128]{2,1,0:T(8,128)} %gather_fusion, pred[48]{0:T(512)(128)(4,1)S(1)} %get-tuple-element.10), kind=kOutput, calls=%fused_computation.5 | convolution fusion | flops 302186496 | bytes 4718640 | tf_op jit(solution)/shard_map/cta,tab->ctb/dot_general | solution.py:44
  19.8 0.9 fusion
  20.8 0.7 copy-done.1
  21.5 0.8 multiply_reduce_fusion
  22.4 35.7 %all-reduce.1 = (f32[16]{0:T(128)S(1)}, f32[16]{0:T(128)S(1)}) all-reduce(f32[16]{0:T(128)S(1)} %get-tuple-element.5, f32[16]{0:T(128)S(1)} %get-tuple-element.4), channel_id=1, replica_groups=mesh['graphs'=2,'rows'=4,'cols'=2,'sub'=2] {'rows','cols','sub'}, use_global_device_ids=true, to_apply=%region_1.2 | all-reduce | flops 32 | bytes 256 | tf_op jit(solution)/shard_map/psum | solution.py:78
  58.1 1.3 fusion.53
  59.4 30.0 %psum.37 = f32[16,16]{1,0:T(8,128)S(1)} all-reduce(f32[16,16]{1,0:T(8,128)S(1)} %fusion.53), channel_id=1, replica_groups=mesh['graphs'=2,'rows'=4,'cols'=2,'sub'=2] {'rows','cols','sub'}, use_global_device_ids=true, to_apply=%region_4.5 | all-reduce | flops 256 | bytes 2048 | tf_op jit(solution)/shard_map/psum | solution.py:85
  89.5 0.7 select_add_fusion.1
  90.3 0.7 fusion.34
  91.0 1.4 cholesky.31
  93.8 1.2 custom-call.12
  95.0 1.3 fusion.32
  96.3 1.8 collective-permute-start.2
  98.1 1.3 collective-permute-start.3
  99.4 2.0 %fusion.20 = f32[48,48]{0,1:T(8,128)} fusion(f32[16,2048]{1,0:T(8,128)} %param.10, f32[16,2048]{1,0:T(8,128)S(1)} %fusion.32, f32[16,2048]{1,0:T(8,128)S(1)} %copy-done.2), kind=kOutput, calls=%fused_computation.26 | convolution fusion | flops 56819712 | bytes 402432 | tf_op jit(solution)/shard_map/dot_general | solution.py:25
  101.5 0.7 copy_bitcast_fusion.1
  102.2 2.3 %gather_fusion.1 = f32[48,16,128]{2,1,0:T(8,128)} fusion(f32[16,32,128]{2,0,1:T(8,128)} %copy_bitcast_fusion.1, s32[1024]{0:T(1024)S(1)} %pad_clamp_fusion), kind=kCustom, calls=%fused_computation.1 | custom fusion | bytes 786624 | tf_op jit(solution)/shard_map/jit(_take)/gather | solution.py:43
  104.5 3.8 %fusion.14 = f32[48,16,128]{2,1,0:T(8,128)S(1)} fusion(f32[48,128,128]{2,1,0:T(8,128)S(1)} %copy-done, f32[48,16,128]{2,1,0:T(8,128)} %gather_fusion.1, pred[48]{0:T(512)(128)(4,1)S(1)} %get-tuple-element.10), kind=kOutput, calls=%fused_computation.20 | convolution fusion | flops 151093248 | bytes 3932208 | tf_op jit(solution)/shard_map/cta,tab->ctb/dot_general | solution.py:44
  109.4 1.5 fusion.6
  110.9 60.5 %all-reduce = (f32[48,48]{0,1:T(8,128)S(1)}, f32[48,48]{0,1:T(8,128)S(1)}) all-reduce(f32[48,48]{0,1:T(8,128)S(1)} %fusion.6, f32[48,48]{0,1:T(8,128)} %fusion.20), channel_id=1, replica_groups=mesh['graphs'=2,'rows'=4,'cols'=2,'sub'=2] {'rows','cols','sub'}, use_global_device_ids=true, to_apply=%region_10.11 | all-reduce | flops 4608 | bytes 36864 | tf_op jit(solution)/shard_map/psum | solution.py:94
  171.7 4.4 %cholesky.65 = f32[48,48]{1,0:T(8,128)S(1)} custom-call(f32[48,48]{1,0:T(8,128)S(1)} %fusion.29), custom_call_target="Cholesky" | custom-call | tf_op jit(solution)/shard_map/jit(cholesky)/cholesky | solution.py:33
  177.4 3.7 %custom-call.15 = f32[1,48,48]{1,2,0:T(8,128)S(1)} custom-call(f32[1,48,48]{2,1,0:T(8,128)S(1)} %fusion.23), custom_call_target="InvertDiagBlocksLowerTriangular" | custom-call | tf_op jit(solution)/shard_map/triangular_solve/custom-call.3 | solution.py:29
  181.4 0.8 fusion.27
  (42 shorter events, 5.8 us)
Async XLA Ops:
  0.6 15.2 %copy-start = (f32[48,128,128]{2,1,0:T(8,128)S(1)}, f32[48,128,128]{2,1,0:T(8,128)}, u32[]{:S(2)}) copy-start(f32[48,128,128]{2,1,0:T(8,128)} %param.11) | copy-start | bytes 9437188
  3.3 8.1 %collective-permute-start = (f32[32,1024]{1,0:T(8,128)}, f32[32,1024]{1,0:T(8,128)}, u32[]{:S(2)}, u32[]{:S(2)}) collective-permute-start(f32[32,1024]{1,0:T(8,128)} %get-tuple-element.14), channel_id=1, source_target_pairs={{0,1},{1,2},{2,3},{3,4},{4,5},{5,6},{6,7},{7,8},{8,9},{9,10},{10,1... | collective-permute-start | bytes 393224 | tf_op jit(solution)/shard_map/ppermute | solution.py:15
  6.4 5.1 %collective-permute-start.1 = (f32[32,1024]{1,0:T(8,128)S(1)}, f32[32,1024]{1,0:T(8,128)}, u32[]{:S(2)}, u32[]{:S(2)}) collective-permute-start(f32[32,1024]{1,0:T(8,128)S(1)} %get-tuple-element.15), channel_id=1, source_target_pairs={{1,0},{2,1},{3,2},{4,3},{5,4},{6,5},{7,6},{8,7},{9,8},{10,9},{11,1... | collective-permute-start | bytes 393224 | tf_op jit(solution)/shard_map/ppermute | solution.py:17
  10.1 1.3 copy-start.6
  15.8 5.7 %copy-start.2 = (f32[16,2048]{1,0:T(8,128)S(1)}, f32[16,2048]{1,0:T(8,128)}, u32[]{:S(2)}) copy-start(f32[16,2048]{1,0:T(8,128)} %param.9) | copy-start | bytes 393220
  20.8 0.7 copy-start.1
  96.3 12.5 %copy-start.3 = (f32[16,2048]{1,0:T(8,128)}, f32[16,2048]{1,0:T(8,128)S(1)}, u32[]{:S(2)}) copy-start(f32[16,2048]{1,0:T(8,128)S(1)} %fusion.32) | copy-start | bytes 393220
  96.3 5.2 %collective-permute-start.2 = (f32[16,1024]{1,0:T(8,128)S(1)}, f32[16,1024]{1,0:T(8,128)S(1)}, u32[]{:S(2)}, u32[]{:S(2)}) collective-permute-start(f32[16,1024]{1,0:T(8,128)S(1)} %get-tuple-element.16), channel_id=1, source_target_pairs={{0,1},{1,2},{2,3},{3,4},{4,5},{5,6},{6,7},{7,8},{8,9},{9,10},{10,1... | collective-permute-start | bytes 196616 | tf_op jit(solution)/shard_map/ppermute | solution.py:15
  98.1 3.4 %collective-permute-start.3 = (f32[16,1024]{1,0:T(8,128)S(1)}, f32[16,1024]{1,0:T(8,128)S(1)}, u32[]{:S(2)}, u32[]{:S(2)}) collective-permute-start(f32[16,1024]{1,0:T(8,128)S(1)} %get-tuple-element.17), channel_id=1, source_target_pairs={{1,0},{2,1},{3,2},{4,3},{5,4},{6,5},{7,6},{8,7},{9,8},{10,9},{11,1... | collective-permute-start | bytes 196616 | tf_op jit(solution)/shard_map/ppermute | solution.py:17
  104.5 67.0 %copy-start.5 = (f32[48]{0:T(128)S(1)}, f32[48]{0:T(128)}, u32[]{:S(2)}) copy-start(f32[48]{0:T(128)} %pad_maximum_fusion.3) | copy-start | bytes 580
  108.8 0.7 copy-start.4
where the time goes:
time: 183 us; the launch traced here: 182 us
  blocking collectives  126 us (69%)
  other arithmetic  21 us (11%)
  matrix products  16.3 us (9%)
  local copies, waits for them, and re-layouts  9.1 us (5%)
  starting transfers between devices  7.44 us (4%)
  between operations  2.15 us (1%)
    psum x1, blocking collectives, body(): lax.psum((inner_products(search, search), inner_products(search, search_i...  60.5 us
    psum x1, blocking collectives, body(): lax.psum((jnp.sum(current_block * x_image, axis=1), jnp.sum(current_block...  35.7 us
    psum x1, blocking collectives, body(): lax.psum(inner_products(residual, residual), ('rows', 'cols', 'sub'))  30 us
    dot_general x2, matrix products, operate(): jnp.einsum('cta,tab->ctb', gathered, adjacency_tiles, precision=lax.Preci...  7.77 us
    another operation x4, other arithmetic, solve_lower(): lax.linalg.triangular_solve(factor, values, left_side=True, lower=True)  6.2 us
    another operation x3, other arithmetic, rayleigh_ritz(): factor_b = jnp.linalg.cholesky(gram_b)  5.06 us
    ppermute x2, starting transfers between devices, extended(): lax.ppermute(tail, axis, [(i, (i + 1) % count) for i in range(ends)])  4.87 us
    dot_general x3, matrix products, inner_products(): return jnp.dot(left, right.T, precision=lax.Precision.HIGHEST)  4.86 us
  transfers between devices with their start and end apart: 4, of which 0 were waited for; matrix products, arithmetic and copies ran while one was open for 2% of the time, Pallas kernels for 0%

commit v1 on v0

--- a/solution.py
+++ b/solution.py
@@ -82,7 +82,8 @@
     quotient = cross_sum / (square_sum + 1e-06)
     residual = jnp.where(frozen_rows[:, None], 0.0, x_image - quotient[:, None] * current_block)
     gram_w = (
-        lax.psum(inner_products(residual, residual), ("rows", "cols", "sub")) / vertex_total
+        jnp.sum(lax.all_gather(inner_products(residual, residual), ("rows", "cols", "sub")), axis=0)
+        / vertex_total
         + frozen_diag
     )
     factor = jnp.linalg.cholesky(gram_w)

time: 183 us -> 172 us (0.940)
  blocking collectives: 126 us -> 114 us
    psum x1 -> x0, blocking collectives: 30 us -> none  [body(): lax.psum(inner_products(residual, residual), ('rows', 'cols', 'sub'))]
    all_gather x0 -> x1, blocking collectives: none -> 17.5 us  [body(): lax.all_gather(inner_products(residual, residual), ('rows', 'cols', 'sub'))]
  transfers between devices with their start and end apart: 4 -> 4, of which waited for: 0 -> 1; matrix products, arithmetic and copies ran while one was open for 2% -> 3% of each run, Pallas kernels for 0% -> 0%
where the time goes in v1:
time: 172 us; the launch traced here: 171 us
  blocking collectives  114 us (66%)
  other arithmetic  20.4 us (12%)
  matrix products  16.3 us (9%)
  local copies, waits for them, and re-layouts  9.18 us (5%)
  starting transfers between devices  7.87 us (5%)
  between operations  2.14 us (1%)
    psum x1, blocking collectives, body(): lax.psum((inner_products(search, search), inner_products(search, search_i...  61.2 us
    psum x1, blocking collectives, body(): lax.psum((jnp.sum(current_block * x_image, axis=1), jnp.sum(current_block...  35.7 us
    all_gather x1, blocking collectives, body(): lax.all_gather(inner_products(residual, residual), ('rows', 'cols', 'sub'))  17.5 us
    dot_general x2, matrix products, operate(): jnp.einsum('cta,tab->ctb', gathered, adjacency_tiles, precision=lax.Preci...  7.77 us
    another operation x4, other arithmetic, solve_lower(): lax.linalg.triangular_solve(factor, values, left_side=True, lower=True)  6.2 us
    ppermute x2, starting transfers between devices, extended(): lax.ppermute(tail, axis, [(i, (i + 1) % count) for i in range(ends)])  5.3 us
    another operation x3, other arithmetic, rayleigh_ritz(): factor_b = jnp.linalg.cholesky(gram_b)  5.06 us
    dot_general x3, matrix products, inner_products(): return jnp.dot(left, right.T, precision=lax.Precision.HIGHEST)  4.87 us
  transfers between devices with their start and end apart: 4, of which 1 were waited for; matrix products, arithmetic and copies ran while one was open for 3% of the time, Pallas kernels for 0%

profile of v1, /device:TPU:0, one launch (start us, length us, event | category | flops | bytes accessed | tf_op | source)
XLA Modules:
  0.0 171.4 jit_solution(10563365705839292605)
XLA Ops:
  0.6 1.1 constant_dynamic-update-slice_fusion.1
  1.7 0.9 constant_dynamic-update-slice_fusion
  2.6 0.7 fusion.51
  3.3 3.0 %collective-permute-start = (f32[32,1024]{1,0:T(8,128)}, f32[32,1024]{1,0:T(8,128)}, u32[]{:S(2)}, u32[]{:S(2)}) collective-permute-start(f32[32,1024]{1,0:T(8,128)} %get-tuple-element.14), channel_id=1, source_target_pairs={{0,1},{1,2},{2,3},{3,4},{4,5},{5,6},{6,7},{7,8},{8,9},{9,10},{10,1... | collective-permute-start | bytes 393224 | tf_op jit(solution)/shard_map/ppermute | solution.py:15
  6.4 1.3 collective-permute-start.1
  7.7 0.7 broadcast_subtract_fusion
  10.1 0.7 compare_and_fusion
  11.5 1.8 %copy_bitcast_fusion = f32[32,32,128]{2,0,1:T(8,128)} fusion(f32[32,1024]{1,0:T(8,128)} %collective-permute-done.1, f32[32,2048]{1,0:T(8,128)S(1)} %constant_dynamic-update-slice_fusion, f32[32,1024]{1,0:T(8,128)} %collective-permute-done), kind=kLoop, calls=%fused_computation.9 | loop fusion | flops 262144 | bytes 1048576 | tf_op jit(solution)/shard_map/reshape | solution.py:42
  13.3 2.5 %gather_fusion = f32[48,32,128]{2,1,0:T(8,128)} fusion(f32[32,32,128]{2,0,1:T(8,128)} %copy_bitcast_fusion, s32[1024]{0:T(1024)S(1)} %pad_clamp_fusion), kind=kCustom, calls=%fused_computation | custom fusion | bytes 1573056 | tf_op jit(solution)/shard_map/jit(_take)/gather | solution.py:43
  15.8 4.0 %convolution_bitcast_fusion = f32[32,48,128]{2,0,1:T(8,128)S(1)} fusion(f32[48,128,128]{2,1,0:T(8,128)S(1)} %copy-done, f32[48,32,128]{2,1,0:T(8,128)} %gather_fusion, pred[48]{0:T(512)(128)(4,1)S(1)} %get-tuple-element.10), kind=kOutput, calls=%fused_computation.2 | convolution fusion | flops 302186496 | bytes 4718640 | tf_op jit(solution)/shard_map/cta,tab->ctb/dot_general | solution.py:44
  19.8 0.9 fusion.1
  20.8 0.7 copy-done.1
  21.5 0.8 multiply_reduce_fusion
  22.4 35.7 %all-reduce.1 = (f32[16]{0:T(128)S(1)}, f32[16]{0:T(128)S(1)}) all-reduce(f32[16]{0:T(128)S(1)} %get-tuple-element.5, f32[16]{0:T(128)S(1)} %get-tuple-element.4), channel_id=1, replica_groups=mesh['graphs'=2,'rows'=4,'cols'=2,'sub'=2] {'rows','cols','sub'}, use_global_device_ids=true, to_apply=%region_1.2 | all-reduce | flops 32 | bytes 256 | tf_op jit(solution)/shard_map/psum | solution.py:78
  58.1 1.3 fusion.50
  59.4 17.5 %all-gather = f32[256,16]{1,0:T(8,128)S(1)} all-gather(f32[16,16]{1,0:T(8,128)S(1)} %fusion.50), channel_id=2, replica_groups=mesh['graphs'=2,'rows'=4,'cols'=2,'sub'=2] {'rows','cols','sub'}, dimensions={0}, use_global_device_ids=true | all-gather | bytes 17408 | tf_op jit(solution)/shard_map/all_gather | solution.py:85
  77.1 0.8 fusion.31
  77.9 1.4 cholesky.31
  80.7 1.2 custom-call.12
  81.9 1.3 fusion.28
  83.2 2.3 %collective-permute-start.2 = (f32[16,1024]{1,0:T(8,128)S(1)}, f32[16,1024]{1,0:T(8,128)S(1)}, u32[]{:S(2)}, u32[]{:S(2)}) collective-permute-start(f32[16,1024]{1,0:T(8,128)S(1)} %get-tuple-element.16), channel_id=1, source_target_pairs={{0,1},{1,2},{2,3},{3,4},{4,5},{5,6},{6,7},{7,8},{8,9},{9,10},{10,1... | collective-permute-start | bytes 196616 | tf_op jit(solution)/shard_map/ppermute | solution.py:15
  85.5 1.3 collective-permute-start.3
  86.8 2.1 %fusion.16 = f32[48,48]{0,1:T(8,128)} fusion(f32[16,2048]{1,0:T(8,128)} %param.10, f32[16,2048]{1,0:T(8,128)S(1)} %fusion.28, f32[16,2048]{1,0:T(8,128)S(1)} %copy-done.2), kind=kOutput, calls=%fused_computation.24 | convolution fusion | flops 56819712 | bytes 402432 | tf_op jit(solution)/shard_map/dot_general | solution.py:25
  88.8 1.1 collective-permute-done.3
  89.9 0.7 copy_bitcast_fusion.1
  90.6 2.3 %gather_fusion.1 = f32[48,16,128]{2,1,0:T(8,128)} fusion(f32[16,32,128]{2,0,1:T(8,128)} %copy_bitcast_fusion.1, s32[1024]{0:T(1024)S(1)} %pad_clamp_fusion), kind=kCustom, calls=%fused_computation.1 | custom fusion | bytes 786624 | tf_op jit(solution)/shard_map/jit(_take)/gather | solution.py:43
  92.9 3.8 %convolution_bitcast_fusion.1 = f32[16,48,128]{2,0,1:T(8,128)S(1)} fusion(f32[48,128,128]{2,1,0:T(8,128)S(1)} %copy-done, f32[48,16,128]{2,1,0:T(8,128)} %gather_fusion.1, pred[48]{0:T(512)(128)(4,1)S(1)} %get-tuple-element.10), kind=kOutput, calls=%fused_computation.3 | convolution fusion | flops 151093248 | bytes 3932208 | tf_op jit(solution)/shard_map/cta,tab->ctb/dot_general | solution.py:44
  97.8 1.5 fusion.4
  99.3 61.2 %all-reduce = (f32[48,48]{0,1:T(8,128)S(1)}, f32[48,48]{0,1:T(8,128)S(1)}) all-reduce(f32[48,48]{0,1:T(8,128)S(1)} %fusion.4, f32[48,48]{0,1:T(8,128)} %fusion.16), channel_id=1, replica_groups=mesh['graphs'=2,'rows'=4,'cols'=2,'sub'=2] {'rows','cols','sub'}, use_global_device_ids=true, to_apply=%region_10.11 | all-reduce | flops 4608 | bytes 36864 | tf_op jit(solution)/shard_map/psum | solution.py:95
  160.8 4.4 %cholesky.65 = f32[48,48]{1,0:T(8,128)S(1)} custom-call(f32[48,48]{1,0:T(8,128)S(1)} %fusion.25), custom_call_target="Cholesky" | custom-call | tf_op jit(solution)/shard_map/jit(cholesky)/cholesky | solution.py:33
  166.5 3.7 %custom-call.15 = f32[1,48,48]{1,2,0:T(8,128)S(1)} custom-call(f32[1,48,48]{2,1,0:T(8,128)S(1)} %fusion.19), custom_call_target="InvertDiagBlocksLowerTriangular" | custom-call | tf_op jit(solution)/shard_map/triangular_solve/custom-call.3 | solution.py:29
  170.5 0.8 fusion.23
  (44 shorter events, 5.9 us)
Async XLA Ops:
  0.6 15.2 %copy-start = (f32[48,128,128]{2,1,0:T(8,128)S(1)}, f32[48,128,128]{2,1,0:T(8,128)}, u32[]{:S(2)}) copy-start(f32[48,128,128]{2,1,0:T(8,128)} %param.11) | copy-start | bytes 9437188
  3.3 8.1 %collective-permute-start = (f32[32,1024]{1,0:T(8,128)}, f32[32,1024]{1,0:T(8,128)}, u32[]{:S(2)}, u32[]{:S(2)}) collective-permute-start(f32[32,1024]{1,0:T(8,128)} %get-tuple-element.14), channel_id=1, source_target_pairs={{0,1},{1,2},{2,3},{3,4},{4,5},{5,6},{6,7},{7,8},{8,9},{9,10},{10,1... | collective-permute-start | bytes 393224 | tf_op jit(solution)/shard_map/ppermute | solution.py:15
  6.4 5.1 %collective-permute-start.1 = (f32[32,1024]{1,0:T(8,128)S(1)}, f32[32,1024]{1,0:T(8,128)}, u32[]{:S(2)}, u32[]{:S(2)}) collective-permute-start(f32[32,1024]{1,0:T(8,128)S(1)} %get-tuple-element.15), channel_id=1, source_target_pairs={{1,0},{2,1},{3,2},{4,3},{5,4},{6,5},{7,6},{8,7},{9,8},{10,9},{11,1... | collective-permute-start | bytes 393224 | tf_op jit(solution)/shard_map/ppermute | solution.py:17
  10.1 1.3 copy-start.6
  15.8 5.7 %copy-start.2 = (f32[16,2048]{1,0:T(8,128)S(1)}, f32[16,2048]{1,0:T(8,128)}, u32[]{:S(2)}) copy-start(f32[16,2048]{1,0:T(8,128)} %param.9) | copy-start | bytes 393220
  20.8 0.7 copy-start.1
  83.2 14.0 %copy-start.3 = (f32[16,2048]{1,0:T(8,128)}, f32[16,2048]{1,0:T(8,128)S(1)}, u32[]{:S(2)}) copy-start(f32[16,2048]{1,0:T(8,128)S(1)} %fusion.28) | copy-start | bytes 393220
  83.2 5.6 %collective-permute-start.2 = (f32[16,1024]{1,0:T(8,128)S(1)}, f32[16,1024]{1,0:T(8,128)S(1)}, u32[]{:S(2)}, u32[]{:S(2)}) collective-permute-start(f32[16,1024]{1,0:T(8,128)S(1)} %get-tuple-element.16), channel_id=1, source_target_pairs={{0,1},{1,2},{2,3},{3,4},{4,5},{5,6},{6,7},{7,8},{8,9},{9,10},{10,1... | collective-permute-start | bytes 196616 | tf_op jit(solution)/shard_map/ppermute | solution.py:15
  85.5 4.4 %collective-permute-start.3 = (f32[16,1024]{1,0:T(8,128)S(1)}, f32[16,1024]{1,0:T(8,128)S(1)}, u32[]{:S(2)}, u32[]{:S(2)}) collective-permute-start(f32[16,1024]{1,0:T(8,128)S(1)} %get-tuple-element.17), channel_id=1, source_target_pairs={{1,0},{2,1},{3,2},{4,3},{5,4},{6,5},{7,6},{8,7},{9,8},{10,9},{11,1... | collective-permute-start | bytes 196616 | tf_op jit(solution)/shard_map/ppermute | solution.py:17
  92.9 67.7 %copy-start.5 = (f32[48]{0:T(128)S(1)}, f32[48]{0:T(128)}, u32[]{:S(2)}) copy-start(f32[48]{0:T(128)} %pad_maximum_fusion.3) | copy-start | bytes 580
  97.2 0.7 copy-start.4
